TPU v7x, 256 devices: a whole 4x4x8 slice. The times are simulated.
256 devices in a mesh: prow: 16 (over y, x), pcol: 16 (over z, core).
Axes of the slice: x: 4, y: 4, z: 8, core: 2. Of those that a mesh axis runs over, the one named last changes fastest.
Arguments:
- matrix: float32 [4, 16, 256, 4, 16, 256], P(None, 'prow', None, None, 'pcol'), may hold values from -6 to 6, as said below
- factor: float32 [4, 16, 256, 4, 16, 256], P(None, 'prow', None, None, 'pcol'), may hold values from -3 to 3, as said below
Outputs:
- reduced: float32 [4, 16, 256, 4, 16, 256], P(None, 'prow', None, None, 'pcol')
Inputs may be any that keep to these rules, and one draw needn't show every extreme that they name: Symmetric matrix stored in its lower triangle: every entry above the diagonal is zero. `factor`: lower triangular with diagonal entries between 1 and 3; every entry above the diagonal is zero.
All inputs are finite; a program needn't handle non-finite values.
Results may differ from a plain program's by a relative error of at most 0.0001.
Values sent between devices are 32-bit elements; how exact they have to be, the bound alone decides.
No kernel may reach another device: no remote copies, remote signals or barrier semaphores. Data moves between devices by JAX's collectives and lax.ppermute only.
A program may use at most 128 MiB of HBM per device.

v0:
```python
import jax
import jax.numpy as jnp
from jax import lax
from jax.sharding import Mesh
from jax.sharding import PartitionSpec as P

BLOCKS = 2
PCOL = ("pcol_0", "pcol_1")
highest = lax.Precision.HIGHEST


def picked_2(value, axis, root):
    return lax.dynamic_index_in_dim(lax.all_gather(value, axis), root, 0, keepdims=False)


def from_root(value, axes, root):
    value = jnp.where(lax.axis_index(axes) == root, value, jnp.zeros_like(value))
    for axis in axes:
        value = lax.psum(value, axis)
    return value


def product(left, right):
    return jnp.dot(left, right, precision=highest, preferred_element_type=jnp.float32)


def product_trans(left, right):
    return lax.dot_general(
        left, right, (((1,), (1,)), ((), ())), precision=highest, preferred_element_type=jnp.float32
    )


def diagonal_core(diag_block, diag_factor, width):
    identity = jnp.eye(width, dtype=jnp.float32)
    inverse = lax.linalg.triangular_solve(diag_factor, identity, left_side=True, lower=True)
    symmetric = diag_block + diag_block.T - jnp.diag(jnp.diagonal(diag_block))
    inner = product_trans(product(inverse, symmetric), inverse)
    return (inverse, 0.5 * (inner + inner.T))


def on_device(matrix, factor):
    row_tiles = matrix.shape[0]
    width = matrix.shape[2]
    col_tiles = matrix.shape[3]
    prow_count = lax.axis_size("prow")
    pcol_count = lax.axis_size(PCOL)
    prow_index = lax.axis_index("prow")
    pcol_index = lax.axis_index(PCOL)
    height = row_tiles * width
    local = matrix.reshape(height, col_tiles * width)
    factor_local = factor.reshape(height, col_tiles * width)
    tile_rows = jnp.arange(row_tiles, dtype=jnp.int32) * prow_count + prow_index
    tile_cols = jnp.arange(col_tiles, dtype=jnp.int32) * pcol_count + pcol_index
    offsets = jnp.arange(width, dtype=jnp.int32)
    elem_rows = (tile_rows[:, None] * width + offsets[None, :]).reshape(height)
    elem_cols = (tile_cols[:, None] * width + offsets[None, :]).reshape(col_tiles * width)
    lower_part = elem_rows[:, None] >= elem_cols[None, :]
    row_tile_of = jnp.repeat(tile_rows, width)[:, None]
    ratio = pcol_count // prow_count
    home = pcol_index % prow_count

    def select_columns(block):
        shaped = block.reshape(col_tiles, ratio, width, width)
        picked = lax.dynamic_index_in_dim(shaped, pcol_index // prow_count, 1, keepdims=False)
        return picked.reshape(col_tiles * width, width)

    for step in range(BLOCKS):
        owner_row = step % prow_count
        owner_col = step % pcol_count
        first = step // pcol_count * width
        diag_start = step // prow_count * width
        panel = local[:, first : first + width]
        factor_panel = factor_local[:, first : first + width]
        diag_block, diag_factor = (
            picked_2(panel[diag_start : diag_start + width], "prow", owner_row),
            picked_2(factor_panel[diag_start : diag_start + width], "prow", owner_row),
        )
        inverse, core = diagonal_core(diag_block, diag_factor, width)
        below = row_tile_of > step
        factor_rows = jnp.where(below, factor_panel, 0.0)
        shared = product(factor_rows, core)
        halfway = jnp.where(below, product_trans(panel, inverse), 0.0) - 0.5 * shared
        finished = halfway - 0.5 * shared
        got_half, got_factor = (
            from_root(halfway, PCOL, owner_col),
            from_root(factor_rows, PCOL, owner_col),
        )
        keeper = prow_index == home
        col_half, col_factor = lax.psum(
            (
                jnp.where(keeper, select_columns(got_half), 0.0),
                jnp.where(keeper, select_columns(got_factor), 0.0),
            ),
            "prow",
        )
        update = product_trans(
            jnp.concatenate([got_half, got_factor], 1), jnp.concatenate([col_factor, col_half], 1)
        )
        local = local - jnp.where(lower_part, update, 0.0)
        current = local[:, first : first + width]
        diag_rows = jnp.tile(jnp.tril(core), (row_tiles, 1))
        column = jnp.where(row_tile_of == step, diag_rows, jnp.where(below, finished, current))
        column = jnp.where(pcol_index == owner_col, column, current)
        local = local.at[:, first : first + width].set(column)
    return local.reshape(row_tiles, 1, width, col_tiles, 1, width)


def solution(mesh):
    torus = Mesh(mesh.devices.reshape(mesh.shape["prow"], 8, 2), ("prow", "pcol_0", "pcol_1"))
    in_specs = (P(None, "prow", None, None, PCOL, None), P(None, "prow", None, None, PCOL, None))
    out_specs = P(None, "prow", None, None, PCOL, None)
    return jax.shard_map(
        on_device, mesh=torus, in_specs=in_specs, out_specs=out_specs, check_vma=False
    )
```

profile of v0, /device:TPU:2, one launch (start us, length us, event | category | flops | bytes accessed | tf_op | source)
XLA Modules:
  0.0 747.6 jit_solution(9152688396294790002)
XLA Ops:
  6.5 14.3 %reduce.9 = f32[4,256,4,256]{3,2,1,0:T(4,128)} reduce(f32[4,1,256,4,1,256]{5,4,3,2,1,0:T(1,128)} %param.8, f32[]{:T(128)} %constant.193), dimensions={1,4}, to_apply=%param.8.reduce_sub_computation | reduce | bytes 8388612 | tf_op args[0]
  20.8 3.2 copy.35
  24.0 2.0 copy-done
  26.8 14.2 %reduce.10 = f32[4,256,4,256]{3,2,1,0:T(4,128)} reduce(f32[4,1,256,4,1,256]{5,4,3,2,1,0:T(1,128)} %param.9, f32[]{:T(128)} %constant.193), dimensions={1,4}, to_apply=%param.9.reduce_sub_computation | reduce | bytes 8388612 | tf_op args[1]
  41.1 3.3 copy.38
  44.4 1.9 copy-done.2
  47.6 2.8 fusion.20
  50.3 36.0 %all-gather.9.cloned.1.call-done = f32[4096,256]{1,0:T(8,128)} async-done(((f32[256,256]{1,0:T(8,128)}), f32[4096,256]{1,0:T(8,128)}) %all-gather.9.cloned.1.call-update) | async-done | bytes 4194320 | tf_op jit(solution)/shard_map/all_gather | solution.py:13
  87.4 57.5 %all-gather.7.cloned.1.call-done = f32[4096,256]{1,0:T(8,128)} async-done(((f32[256,256]{1,0:T(8,128)}), f32[4096,256]{1,0:T(8,128)}) %all-gather.7.cloned.1.call-update) | async-done | bytes 4194320 | tf_op jit(solution)/shard_map/all_gather | solution.py:13
  144.9 1.8 slice_select_fusion.4
  146.8 4.1 while.6
  147.4 1.4 bitcast_dynamic-update-slice_fusion.4
  149.5 1.4 bitcast_dynamic-update-slice_fusion.4
  150.9 19.7 %custom-call.8 = f32[2,128,128]{1,2,0:T(8,128)S(1)} custom-call(f32[2,128,128]{2,1,0:T(8,128)S(1)} %get-tuple-element.44), custom_call_target="InvertDiagBlocksLowerTriangular" | custom-call | tf_op jit(solution)/shard_map/triangular_solve/custom-call.1 | solution.py:35
  171.6 2.3 gather_fusion
  174.0 1.4 fusion.31
  175.9 2.3 convolution_multiply_fusion.1
  178.6 2.3 fusion.15
  180.9 1.3 copy.22
  182.2 2.3 broadcast_select_fusion.5
  184.6 80.9 %all-reduce.19.cloned.1.call-done = (f32[1024,256]{1,0:T(8,128)}, f32[1024,256]{1,0:T(8,128)}) async-done(((f32[1024,256]{1,0:T(8,128)}, f32[1024,256]{1,0:T(8,128)}), (f32[1024,256]{1,0:T(8,128)}, f32[1024,256]{1,0:T(8,128)})) %all-reduce.19.cloned.1.call-update) | async-done | bytes 2097168 | tf_op jit(solution)/shard_map/psum | solution.py:19
  265.6 33.6 %all-reduce.23.cloned.1.call-done = (f32[1024,256]{1,0:T(8,128)}, f32[1024,256]{1,0:T(8,128)}) async-done(((f32[1024,256]{1,0:T(8,128)}, f32[1024,256]{1,0:T(8,128)}), (f32[1024,256]{1,0:T(8,128)}, f32[1024,256]{1,0:T(8,128)})) %all-reduce.23.cloned.1.call-update) | async-done | bytes 2097168 | tf_op jit(solution)/shard_map/psum | solution.py:19
  300.2 1.1 broadcast_select_fusion.4
  302.8 1.3 copy.39
  304.0 101.4 %all-reduce.15.cloned.1.call-done = (f32[1024,256]{1,0:T(8,128)}, f32[1024,256]{1,0:T(8,128)}) async-done(((f32[1024,256]{1,0:T(8,128)}, f32[1024,256]{1,0:T(8,128)}), (f32[1024,256]{1,0:T(8,128)}, f32[1024,256]{1,0:T(8,128)})) %all-reduce.15.cloned.1.call-update) | async-done | bytes 2097168 | tf_op jit(solution)/shard_map/psum | solution.py:89
  405.4 10.8 %fusion = f32[1024,1024]{1,0:T(8,128)S(1)} fusion(f32[1024,1024]{1,0:T(8,128)} %bitcast.90, f32[1024,256]{1,0:T(8,128)} %get-tuple-element.72, f32[1024,256]{1,0:T(8,128)} %get-tuple-element.73, f32[1024,256]{1,0:T(8,128)} %get-tuple-element.64, f32[1024,256]{1,0:T(8,128)} %get-tuple-element.65, s32[1024]{0:T(1024)S(1)} %bitcast.99, s32[1024]{0:T(1024)S(1)} %bitcast.101), kind=kOutput, calls=%fused_computation.8 | convolution fusion | flops 6446645248 | bytes 12591104 | tf_op jit(solution)/shard_map/dot_general | solution.py:28
  416.2 2.0 copy-done.1
  418.3 1.3 copy.25
  419.7 2.7 select_select_fusion.1
  423.4 5.9 while.7
  424.1 2.3 bitcast_dynamic-update-slice_fusion.5
  427.1 2.2 bitcast_dynamic-update-slice_fusion.5
  429.3 19.7 %custom-call.9 = f32[2,128,128]{1,2,0:T(8,128)S(1)} custom-call(f32[2,128,128]{2,1,0:T(8,128)S(1)} %get-tuple-element.45), custom_call_target="InvertDiagBlocksLowerTriangular" | custom-call | tf_op jit(solution)/shard_map/triangular_solve/custom-call.1 | solution.py:35
  449.3 1.2 convolution_subtract_fusion
  450.9 33.9 %all-gather.11.cloned.1.call-done = f32[4096,256]{0,1:T(8,128)} async-done(((f32[256,256]{0,1:T(8,128)}), f32[4096,256]{0,1:T(8,128)}) %all-gather.11.cloned.1.call-update) | async-done | bytes 4194320 | tf_op jit(solution)/shard_map/all_gather | solution.py:13
  485.9 2.4 gather_fusion.1
  488.3 1.4 fusion.27
  490.9 2.3 convolution_multiply_fusion
  493.2 3.9 broadcast_select_fusion.2
  497.2 82.1 %all-reduce.17.cloned.1.call-done = (f32[1024,256]{1,0:T(8,128)}, f32[1024,256]{1,0:T(8,128)}) async-done(((f32[1024,256]{1,0:T(8,128)}, f32[1024,256]{1,0:T(8,128)}), (f32[1024,256]{1,0:T(8,128)}, f32[1024,256]{1,0:T(8,128)})) %all-reduce.17.cloned.1.call-update) | async-done | bytes 2097168 | tf_op jit(solution)/shard_map/psum | solution.py:19
  579.6 33.4 %all-reduce.21.cloned.1.call-done = (f32[1024,256]{1,0:T(8,128)}, f32[1024,256]{1,0:T(8,128)}) async-done(((f32[1024,256]{1,0:T(8,128)}, f32[1024,256]{1,0:T(8,128)}), (f32[1024,256]{1,0:T(8,128)}, f32[1024,256]{1,0:T(8,128)})) %all-reduce.21.cloned.1.call-update) | async-done | bytes 2097168 | tf_op jit(solution)/shard_map/psum | solution.py:19
  613.1 1.1 broadcast_select_fusion
  615.3 1.3 copy.30
  616.6 2.3 constant_dynamic-update-slice_fusion
  620.0 99.2 %all-reduce.13.cloned.1.call-done = (f32[1024,256]{1,0:T(8,128)}, f32[1024,256]{1,0:T(8,128)}) async-done(((f32[1024,256]{1,0:T(8,128)}, f32[1024,256]{1,0:T(8,128)}), (f32[1024,256]{1,0:T(8,128)}, f32[1024,256]{1,0:T(8,128)})) %all-reduce.13.cloned.1.call-update) | async-done | bytes 2097168 | tf_op jit(solution)/shard_map/psum | solution.py:89
  719.3 10.9 %fusion.1 = f32[1024,1024]{1,0:T(8,128)} fusion(f32[1024,1024]{1,0:T(8,128)} %constant_dynamic-update-slice_fusion, f32[1024,256]{1,0:T(8,128)} %get-tuple-element.70, f32[1024,256]{1,0:T(8,128)} %get-tuple-element.71, f32[1024,256]{1,0:T(8,128)} %get-tuple-element.62, f32[1024,256]{1,0:T(8,128)} %get-tuple-element.63, s32[1024]{0:T(1024)S(1)} %bitcast.100, ...), kind=kOutput, calls=%fused_computation.9 | convolution fusion | flops 6446645248 | bytes 12591104 | tf_op jit(solution)/shard_map/dot_general | solution.py:28
  730.1 3.3 fusion.17
  733.5 7.6 %reshape.220 = f32[4,1,256,4,1,256]{5,4,3,2,1,0:T(1,128)} reshape(f32[1024,1024]{1,0:T(8,128)} %fusion.17) | data formatting | bytes 8388608 | tf_op jit(solution)/shard_map/reshape | solution.py:105
  (81 shorter events, 17.0 us)
Async XLA Ops:
  6.5 79.8 %all-gather.9.cloned.1.call-start = ((), (), s32[]{:S(2)}) async-start(), calls=%async_computation.1 | async-start | bytes 4456448 | tf_op jit(solution)/shard_map/all_gather | solution.py:13
  24.0 2.0 copy-start
  26.8 118.1 %all-gather.7.cloned.1.call-start = ((), (), s32[]{:S(2)}) async-start(), calls=%async_computation | async-start | bytes 4456448 | tf_op jit(solution)/shard_map/all_gather | solution.py:13
  44.4 1.9 copy-start.2
  47.1 218.4 %all-reduce.19.cloned.1.call-start = ((), (), s32[]{:S(2)}) async-start(), calls=%async_computation.6 | async-start | bytes 4194304 | tf_op jit(solution)/shard_map/psum | solution.py:19
  184.5 114.6 %all-reduce.23.cloned.1.call-start = ((), (), s32[]{:S(2)}) async-start(), calls=%async_computation.8 | async-start | bytes 4194304 | tf_op jit(solution)/shard_map/psum | solution.py:19
  265.5 139.9 %all-reduce.15.cloned.1.call-start = ((), (), s32[]{:S(2)}) async-start(), calls=%async_computation.4 | async-start | bytes 4194304 | tf_op jit(solution)/shard_map/psum | solution.py:89
  301.3 183.5 %all-gather.11.cloned.1.call-start = ((), (), s32[]{:S(2)}) async-start(), calls=%async_computation.2 | async-start | bytes 4456448 | tf_op jit(solution)/shard_map/all_gather | solution.py:13
  416.2 2.0 copy-start.1
  423.1 156.2 %all-reduce.17.cloned.1.call-start = ((), (), s32[]{:S(2)}) async-start(), calls=%async_computation.5 | async-start | bytes 4194304 | tf_op jit(solution)/shard_map/psum | solution.py:19
  450.9 39.2 %copy-start.4 = (f32[128,256]{1,0:T(8,128)}, f32[128,256]{1,0:T(8,128)S(1)}, u32[]{:S(2)}) copy-start(f32[128,256]{1,0:T(8,128)S(1)} %fusion.51) | copy-start | bytes 393220
  490.2 0.7 copy-start.3
  497.1 115.9 %all-reduce.21.cloned.1.call-start = ((), (), s32[]{:S(2)}) async-start(), calls=%async_computation.7 | async-start | bytes 4194304 | tf_op jit(solution)/shard_map/psum | solution.py:19
  579.3 140.0 %all-reduce.13.cloned.1.call-start = ((), (), s32[]{:S(2)}) async-start(), calls=%async_computation.3 | async-start | bytes 4194304 | tf_op jit(solution)/shard_map/psum | solution.py:89
Sparse Core Ops, SparseCore 0:
  26.9 59.3 all-gather.8
  88.7 56.1 all-gather.6
  184.6 80.7 all-reduce.18
  268.0 31.1 all-reduce.22
  302.3 103.0 all-reduce.14
  423.2 61.5 all-gather.10
  497.2 81.9 all-reduce.16
  581.9 31.1 all-reduce.20
  616.4 102.8 all-reduce.12
where the time goes:
time: 749 us; the launch traced here: 748 us
  waiting for transfers between devices  558 us (74%)
  other arithmetic  86.9 us (12%)
  local copies, waits for them, and re-layouts  48.9 us (7%)
  matrix products  38.8 us (5%)
  between operations  13.6 us (2%)
    psum x4, waiting for transfers between devices, from_root(): value = lax.psum(value, axis)  230 us
    psum x2, waiting for transfers between devices, on_device(): lax.psum((jnp.where(keeper, select_columns(got_half), 0.0), jnp.where(kee...  201 us
    all_gather x3, waiting for transfers between devices, picked_2(): lax.all_gather(value, axis)  127 us
    another operation x4, other arithmetic, diagonal_core(): lax.linalg.triangular_solve(diag_factor, identity, left_side=True, lower=...  41.1 us
    dot_general x6, matrix products, product_trans(): lax.dot_general(left, right, (((1,), (1,)), ((), ())), precision=highest,...  28.7 us
    unnamed x4, other arithmetic  28.7 us
  transfers between devices with their start and end apart: 9, of which 9 were waited for; matrix products, arithmetic and copies ran while one was open for 8% of the time, Pallas kernels for 0%

commit v1 on v0

--- a/solution.py
+++ b/solution.py
@@ -16,7 +16,8 @@
 def from_root(value, axes, root):
     value = jnp.where(lax.axis_index(axes) == root, value, jnp.zeros_like(value))
     for axis in axes:
-        value = lax.psum(value, axis)
+        terms = lax.all_gather(value, axis, axis=0, tiled=False)
+        value = terms.sum(axis=0)
     return value
 
 

time: 749 us -> 956 us (1.28)
  waiting for transfers between devices: 558 us -> 668 us
  local copies, waits for them, and re-layouts: 48.9 us -> 119 us
  other arithmetic: 86.9 us -> 106 us
    all_gather x0 -> x8, waiting for transfers between devices: none -> 332 us  [from_root(): terms = lax.all_gather(value, axis, axis=0, tiled=False)]
    psum x4 -> x0, waiting for transfers between devices: 230 us -> none  [from_root(): value = lax.psum(value, axis)]
    unnamed x15 -> x30, local copies, waits for them, and re-layouts: 14.5 us -> 57.7 us
    reduce_sum x0 -> x8, other arithmetic: none -> 20.4 us  [from_root(): value = terms.sum(axis=0)]
    all_gather x0 -> x4, local copies, waits for them, and re-layouts: none -> 11.6 us  [from_root(): terms = lax.all_gather(value, axis, axis=0, tiled=False)]
  transfers between devices with their start and end apart: 9 -> 13, of which waited for: 9 -> 13; matrix products, arithmetic and copies ran while one was open for 8% -> 18% of each run, Pallas kernels for 0% -> 0%
where the time goes in v1:
time: 956 us; the launch traced here: 948 us
  waiting for transfers between devices  668 us (70%)
  local copies, waits for them, and re-layouts  119 us (12%)
  other arithmetic  106 us (11%)
  matrix products  38 us (4%)
  between operations  14.1 us (1%)
    all_gather x8, waiting for transfers between devices, from_root(): terms = lax.all_gather(value, axis, axis=0, tiled=False)  332 us
    psum x2, waiting for transfers between devices, on_device(): lax.psum((jnp.where(keeper, select_columns(got_half), 0.0), jnp.where(kee...  200 us
    all_gather x3, waiting for transfers between devices, picked_2(): lax.all_gather(value, axis)  135 us
    unnamed x30, local copies, waits for them, and re-layouts  57.7 us
    another operation x4, other arithmetic, diagonal_core(): lax.linalg.triangular_solve(diag_factor, identity, left_side=True, lower=...  41.1 us
    dot_general x6, matrix products, product_trans(): lax.dot_general(left, right, (((1,), (1,)), ((), ())), precision=highest,...  29.2 us
    unnamed x4, other arithmetic  28.6 us
    reduce_sum x8, other arithmetic, from_root(): value = terms.sum(axis=0)  20.4 us
  transfers between devices with their start and end apart: 13, of which 13 were waited for; matrix products, arithmetic and copies ran while one was open for 18% of the time, Pallas kernels for 0%

profile of v1, /device:TPU:2, one launch (start us, length us, event | category | flops | bytes accessed | tf_op | source)
XLA Modules:
  0.0 947.6 jit_solution(7994547202168623907)
XLA Ops:
  6.5 14.3 %reduce.10 = f32[4,256,4,256]{3,2,1,0:T(4,128)} reduce(f32[4,1,256,4,1,256]{5,4,3,2,1,0:T(1,128)} %param.8, f32[]{:T(128)} %constant.193), dimensions={1,4}, to_apply=%param.8.reduce_sub_computation | reduce | bytes 8388612 | tf_op args[0]
  20.8 5.1 copy.123
  26.0 5.3 copy.105
  33.0 14.2 %reduce.9 = f32[4,256,4,256]{3,2,1,0:T(4,128)} reduce(f32[4,1,256,4,1,256]{5,4,3,2,1,0:T(1,128)} %param.9, f32[]{:T(128)} %constant.193), dimensions={1,4}, to_apply=%param.9.reduce_sub_computation | reduce | bytes 8388612 | tf_op args[1]
  47.2 3.3 copy.126
  57.8 39.8 %all-gather.25.cloned.1.call-done = f32[4096,256]{0,1:T(8,128)} async-done(((f32[256,256]{0,1:T(8,128)}), f32[4096,256]{0,1:T(8,128)}) %all-gather.25.cloned.1.call-update) | async-done | bytes 4194320 | tf_op jit(solution)/shard_map/all_gather | solution.py:13
  98.7 62.6 %all-gather.23.cloned.1.call-done = f32[4096,256]{0,1:T(8,128)} async-done(((f32[256,256]{0,1:T(8,128)}), f32[4096,256]{0,1:T(8,128)}) %all-gather.23.cloned.1.call-update) | async-done | bytes 4194320 | tf_op jit(solution)/shard_map/all_gather | solution.py:13
  163.2 4.1 while.6
  167.3 19.7 %custom-call.8 = f32[2,128,128]{1,2,0:T(8,128)S(1)} custom-call(f32[2,128,128]{2,1,0:T(8,128)S(1)} %get-tuple-element.44), custom_call_target="InvertDiagBlocksLowerTriangular" | custom-call | tf_op jit(solution)/shard_map/triangular_solve/custom-call.1 | solution.py:36
  187.0 2.4 gather_fusion
  193.5 3.7 broadcast_select_fusion.5
  197.4 59.6 %all-gather.31.cloned.1.call-done = f32[8192,256]{0,1:T(8,128)} async-done(((f32[1024,256]{0,1:T(8,128)}), f32[8192,256]{0,1:T(8,128)}) %all-gather.31.cloned.1.call-update) | async-done | bytes 8388624 | tf_op jit(solution)/shard_map/all_gather | solution.py:19
  257.0 10.9 %copy.128 = f32[32,8,8,1024]{3,2,1,0:T(8,128)S(1)} copy(f32[32,8,8,1024]{3,1,2,0:T(8,128)} %bitcast.119) | data formatting | bytes 16777216
  268.0 3.0 bitcast_reduce_fusion.2
  271.3 80.0 %all-gather.27.cloned.1.call-done = f32[8192,256]{0,1:T(8,128)} async-done(((f32[1024,256]{0,1:T(8,128)}), f32[8192,256]{0,1:T(8,128)}) %all-gather.27.cloned.1.call-update) | async-done | bytes 8388624 | tf_op jit(solution)/shard_map/all_gather | solution.py:19
  351.3 10.9 %copy.127 = f32[32,8,8,1024]{3,2,1,0:T(8,128)S(1)} copy(f32[32,8,8,1024]{3,1,2,0:T(8,128)} %bitcast.121) | data formatting | bytes 16777216
  362.3 2.9 bitcast_reduce_fusion.3
  367.5 2.9 copy.108
  374.7 11.7 %all-gather.29.cloned.1.call-done = f32[2048,256]{0,1:T(8,128)} async-done(((f32[1024,256]{0,1:T(8,128)}), f32[2048,256]{0,1:T(8,128)}) %all-gather.29.cloned.1.call-update) | async-done | bytes 2097168 | tf_op jit(solution)/shard_map/all_gather | solution.py:19
  386.4 2.9 copy.107
  389.3 2.8 reduce_sum.73
  392.1 2.5 copy.86
  399.1 99.4 %all-reduce.7.cloned.1.call-done = (f32[1024,256]{0,1:T(8,128)}, f32[1024,256]{0,1:T(8,128)}) async-done(((f32[1024,256]{0,1:T(8,128)}, f32[1024,256]{0,1:T(8,128)}), (f32[1024,256]{0,1:T(8,128)}, f32[1024,256]{0,1:T(8,128)})) %all-reduce.7.cloned.1.call-update) | async-done | bytes 2097168 | tf_op jit(solution)/shard_map/psum | solution.py:90
  498.5 10.8 %fusion = f32[1024,1024]{0,1:T(8,128)} fusion(f32[1024,1024]{0,1:T(8,128)} %copy.105, f32[1024,256]{1,0:T(8,128)S(1)} %reduce_sum.75, f32[1024,256]{1,0:T(8,128)} %reduce_sum.73, f32[1024,256]{0,1:T(8,128)} %get-tuple-element.88, f32[1024,256]{0,1:T(8,128)} %get-tuple-element.89, s32[1024]{0:T(1024)S(1)} %bitcast.133, s32[1024]{0:T(1024)S(1)} %bitcast.135), kind=kOutput, calls=%fused_computation.12 | convolution fusion | flops 6446645248 | bytes 12591104 | tf_op jit(solution)/shard_map/dot_general | solution.py:29
  509.4 3.3 constant_dynamic-update-slice_fusion
  514.7 6.0 while.7
  515.4 2.3 dynamic-slice.30
  518.4 2.2 dynamic-slice.30
  520.8 19.7 %custom-call.9 = f32[2,128,128]{1,2,0:T(8,128)S(1)} custom-call(f32[2,128,128]{2,1,0:T(8,128)S(1)} %get-tuple-element.45), custom_call_target="InvertDiagBlocksLowerTriangular" | custom-call | tf_op jit(solution)/shard_map/triangular_solve/custom-call.1 | solution.py:36
  542.2 32.9 %all-gather.35.cloned.1.call-done = f32[4096,256]{0,1:T(8,128)} async-done(((f32[256,256]{0,1:T(8,128)}), f32[4096,256]{0,1:T(8,128)}) %all-gather.35.cloned.1.call-update) | async-done | bytes 4194320 | tf_op jit(solution)/shard_map/all_gather | solution.py:13
  576.3 2.4 gather_fusion.1
  581.3 2.1 convolution_multiply_fusion
  583.4 3.4 broadcast_select_fusion.2
  587.1 83.7 %all-gather.41.cloned.1.call-done = f32[8192,256]{0,1:T(8,128)} async-done(((f32[1024,256]{0,1:T(8,128)}), f32[8192,256]{0,1:T(8,128)}) %all-gather.41.cloned.1.call-update) | async-done | bytes 8388624 | tf_op jit(solution)/shard_map/all_gather | solution.py:19
  670.8 10.9 %copy.131 = f32[32,8,8,1024]{3,2,1,0:T(8,128)S(1)} copy(f32[32,8,8,1024]{3,1,2,0:T(8,128)} %bitcast.120) | data formatting | bytes 16777216
  681.7 3.0 bitcast_reduce_fusion
  685.1 80.1 %all-gather.37.cloned.1.call-done = f32[8192,256]{0,1:T(8,128)} async-done(((f32[1024,256]{0,1:T(8,128)}), f32[8192,256]{0,1:T(8,128)}) %all-gather.37.cloned.1.call-update) | async-done | bytes 8388624 | tf_op jit(solution)/shard_map/all_gather | solution.py:19
  765.1 10.9 %copy.130 = f32[32,8,8,1024]{3,2,1,0:T(8,128)S(1)} copy(f32[32,8,8,1024]{3,1,2,0:T(8,128)} %bitcast.122) | data formatting | bytes 16777216
  776.1 2.9 bitcast_reduce_fusion.1
  779.4 2.1 all-gather.43.cloned.1.call-done
  781.5 2.9 copy.110
  787.6 12.7 %all-gather.39.cloned.1.call-done = f32[2048,256]{0,1:T(8,128)} async-done(((f32[1024,256]{0,1:T(8,128)}), f32[2048,256]{0,1:T(8,128)}) %all-gather.39.cloned.1.call-update) | async-done | bytes 2097168 | tf_op jit(solution)/shard_map/all_gather | solution.py:19
  800.4 2.9 copy.109
  810.0 100.3 %all-reduce.5.cloned.1.call-done = (f32[1024,256]{0,1:T(8,128)}, f32[1024,256]{0,1:T(8,128)}) async-done(((f32[1024,256]{0,1:T(8,128)}, f32[1024,256]{0,1:T(8,128)}), (f32[1024,256]{0,1:T(8,128)}, f32[1024,256]{0,1:T(8,128)})) %all-reduce.5.cloned.1.call-update) | async-done | bytes 2097168 | tf_op jit(solution)/shard_map/psum | solution.py:90
  910.3 10.5 %fusion.1 = f32[1024,1024]{0,1:T(8,128)} fusion(f32[1024,1024]{0,1:T(8,128)} %get-tuple-element.90, f32[1024,256]{1,0:T(8,128)S(1)} %reduce_sum.79, f32[1024,256]{1,0:T(8,128)S(1)} %reduce_sum.77, f32[1024,256]{0,1:T(8,128)} %get-tuple-element.86, f32[1024,256]{0,1:T(8,128)} %get-tuple-element.87, s32[1024]{0:T(1024)S(1)} %bitcast.134, s32[1024]{0:T(1024)S(1)} %bitcast.136), kind=kOutput, calls=%fused_computation.13 | convolution fusion | flops 6446645248 | bytes 12591104 | tf_op jit(solution)/shard_map/dot_general | solution.py:29
  920.9 3.3 fusion.17
  924.1 5.6 reshape.168
  929.8 10.9 %copy.99 = f32[4,1,256,4,1,256]{5,4,3,2,1,0:T(1,128)} copy(f32[4,1,256,4,1,256]{2,0,5,3,4,1:T(4,128)} %reshape.168) | data formatting | bytes 8388608 | tf_op jit(solution)/shard_map/reshape | solution.py:106
  (130 shorter events, 51.1 us)
Async XLA Ops:
  6.5 91.1 %all-gather.25.cloned.1.call-start = ((), (), s32[]{:S(2)}) async-start(), calls=%async_computation.1 | async-start | bytes 4456448 | tf_op jit(solution)/shard_map/all_gather | solution.py:13
  33.0 128.3 %all-gather.23.cloned.1.call-start = ((), (), s32[]{:S(2)}) async-start(), calls=%async_computation | async-start | bytes 4456448 | tf_op jit(solution)/shard_map/all_gather | solution.py:13
  50.6 1.9 copy-start
  53.4 203.6 %all-gather.31.cloned.1.call-start = ((), (), s32[]{:S(2)}) async-start(), calls=%async_computation.4 | async-start | bytes 9437184 | tf_op jit(solution)/shard_map/all_gather | solution.py:19
  56.9 294.4 %all-gather.27.cloned.1.call-start = ((), (), s32[]{:S(2)}) async-start(), calls=%async_computation.2 | async-start | bytes 9437184 | tf_op jit(solution)/shard_map/all_gather | solution.py:19
  57.7 134.4 %copy-start.6 = (f32[256,256]{1,0:T(8,128)}, f32[256,256]{1,0:T(8,128)S(1)}, u32[]{:S(2)}) copy-start(f32[256,256]{1,0:T(8,128)S(1)} %fusion.39) | copy-start | bytes 786436
  192.3 75.7 %copy-start.5 = (f32[256,256]{0,1:T(8,128)}, f32[256,256]{0,1:T(8,128)S(1)}, u32[]{:S(2)}) copy-start(f32[256,256]{0,1:T(8,128)S(1)} %copy.81) | copy-start | bytes 786436
  197.2 170.4 %all-gather.33.cloned.1.call-start = ((), (), s32[]{:S(2)}) async-start(), calls=%async_computation.5 | async-start | bytes 3145728 | tf_op jit(solution)/shard_map/all_gather | solution.py:19
  271.0 115.4 %all-gather.29.cloned.1.call-start = ((), (), s32[]{:S(2)}) async-start(), calls=%async_computation.3 | async-start | bytes 3145728 | tf_op jit(solution)/shard_map/all_gather | solution.py:19
  365.2 133.3 %all-reduce.7.cloned.1.call-start = ((), (), s32[]{:S(2)}) async-start(), calls=%async_computation.12 | async-start | bytes 4194304 | tf_op jit(solution)/shard_map/psum | solution.py:90
  395.8 179.4 %all-gather.35.cloned.1.call-start = ((), (), s32[]{:S(2)}) async-start(), calls=%async_computation.6 | async-start | bytes 4456448 | tf_op jit(solution)/shard_map/all_gather | solution.py:13
  498.5 10.8 %copy-start.1 = (f32[32,8,4,256]{3,1,2,0:T(8,128)S(1)}, f32[32,8,4,256]{3,1,2,0:T(8,128)}, u32[]{:S(2)}) copy-start(f32[32,8,4,256]{3,1,2,0:T(8,128)} %copy.129) | copy-start | bytes 3145732
  498.5 10.8 %copy-start.2 = (f32[1024,256]{0,1:T(8,128)S(1)}, f32[1024,256]{0,1:T(8,128)}, u32[]{:S(2)}) copy-start(f32[1024,256]{0,1:T(8,128)} %get-tuple-element.101) | copy-start | bytes 3145732
  509.4 31.1 %copy-start.7 = (f32[256,256]{1,0:T(8,128)S(1)}, f32[256,256]{1,0:T(8,128)}, u32[]{:S(2)}) copy-start(f32[256,256]{1,0:T(8,128)} %copy-done.6) | copy-start | bytes 786436
  513.4 157.4 %all-gather.41.cloned.1.call-start = ((), (), s32[]{:S(2)}) async-start(), calls=%async_computation.9 | async-start | bytes 9437184 | tf_op jit(solution)/shard_map/all_gather | solution.py:19
  514.2 251.0 %all-gather.37.cloned.1.call-start = ((), (), s32[]{:S(2)}) async-start(), calls=%async_computation.7 | async-start | bytes 9437184 | tf_op jit(solution)/shard_map/all_gather | solution.py:19
  542.2 38.2 %copy-start.8 = (f32[128,256]{1,0:T(8,128)}, f32[128,256]{1,0:T(8,128)S(1)}, u32[]{:S(2)}) copy-start(f32[128,256]{1,0:T(8,128)S(1)} %fusion.51) | copy-start | bytes 393220
  586.8 194.7 %all-gather.43.cloned.1.call-start = ((), (), s32[]{:S(2)}) async-start(), calls=%async_computation.10 | async-start | bytes 3145728 | tf_op jit(solution)/shard_map/all_gather | solution.py:19
  684.8 115.6 %all-gather.39.cloned.1.call-start = ((), (), s32[]{:S(2)}) async-start(), calls=%async_computation.8 | async-start | bytes 3145728 | tf_op jit(solution)/shard_map/all_gather | solution.py:19
  779.1 131.3 %all-reduce.5.cloned.1.call-start = ((), (), s32[]{:S(2)}) async-start(), calls=%async_computation.11 | async-start | bytes 4194304 | tf_op jit(solution)/shard_map/psum | solution.py:90
  910.3 10.5 %copy-start.3 = (f32[32,8,4,256]{3,1,2,0:T(8,128)S(1)}, f32[32,8,4,256]{3,1,2,0:T(8,128)}, u32[]{:S(2)}) copy-start(f32[32,8,4,256]{3,1,2,0:T(8,128)} %copy.132) | copy-start | bytes 3145732
  910.3 10.5 %copy-start.4 = (f32[1024,256]{0,1:T(8,128)S(1)}, f32[1024,256]{0,1:T(8,128)}, u32[]{:S(2)}) copy-start(f32[1024,256]{0,1:T(8,128)} %get-tuple-element.103) | copy-start | bytes 3145732
Sparse Core Ops, SparseCore 0:
  33.1 64.4 all-gather.24
  100.0 61.2 all-gather.22
  163.1 93.8 all-gather.30
  258.7 92.6 all-gather.26
  353.0 14.4 all-gather.32
  369.2 17.1 all-gather.28
  395.9 102.5 all-reduce.6
  513.6 61.5 all-gather.34
  577.0 93.7 all-gather.40
  672.4 92.6 all-gather.36
  766.9 14.4 all-gather.42
  783.1 17.1 all-gather.38
  807.7 102.6 all-reduce.4
